TPU v7x, 256 devices: a whole 4x4x8 slice. The times are simulated.
256 devices in a mesh: seq: 32 (over x, z_lo, core), head: 8 (over y, z_hi).
Axes of the slice: x: 4, y: 4, z: 8 (z_hi: 2, z_lo: 4; z = z_hi * 4 + z_lo), core: 2. Of those that a mesh axis runs over, the one named last changes fastest.
Arguments:
- tokens: bfloat16 [16384, 1024], P('seq'), may hold values from -6 to 6
- mem_query_w: bfloat16 [1024, 1024], P(None, 'head'), may hold values from -0.1875 to 0.1875
- mem_key_w: bfloat16 [1024, 1024], P(None, 'head'), may hold values from -0.1875 to 0.1875
- mem_value_w: bfloat16 [1024, 1024], P(None, 'head'), may hold values from -0.1875 to 0.1875
- mem_in: float32 [1024, 1024], P(None, 'head'), may hold values from -0.1875 to 0.1875
- mem_out: float32 [1024, 1024], P('head'), may hold values from -0.1875 to 0.1875
- forget_levels: float32 [16, 1024], P(None, 'head'), may hold values from 0.003 to 0.3
- momentum_levels: float32 [16, 1024], P(None, 'head'), may hold values from 0.2 to 0.9
- step_levels: float32 [16, 1024], P(None, 'head'), may hold values from 0.02 to 0.2
- plan: int32 [32], P('seq'), may hold values from 0 to 15
- norm_gain: float32 [1024], replicated, may hold values from 0.5 to 1.5
- attn_query_w: bfloat16 [1024, 1024], P(None, 'head'), may hold values from -1 to 1
- attn_key_w: bfloat16 [1024, 1024], P(None, 'head'), may hold values from -4 to 4
- attn_value_w: bfloat16 [1024, 1024], P(None, 'head'), may hold values from -0.1875 to 0.1875
- attn_out_w: bfloat16 [1024, 1024], P('head'), may hold values from -0.25 to 0.25
Outputs:
- layer_out: bfloat16 [16384, 1024], P('seq', 'head')
All inputs are finite; a program needn't handle non-finite values.
Results may differ from a plain program's by a relative error of at most 0.014.
Values may be sent and summed in bfloat16 or wider, within the bound.
A program may use at most 128 MiB of HBM per device.

v0:
```python
import jax
import jax.numpy as jnp
from jax import lax
from jax.sharding import Mesh
from jax.sharding import PartitionSpec as P

HEAD_DIM = 64
SPAN = 8
SEQ = ("seq_0", "seq_1", "seq_2")
epsilon = 1e-06


def split_up(value, dim, length):
    before, after = (value.shape[:dim], value.shape[dim + 1 :])
    return jnp.moveaxis(value.reshape(*before, length, -1, *after), dim, 0)


def sent_and_summed(value, axis, dim):
    length = lax.axis_size(axis)
    blocks = lax.all_to_all(split_up(value, dim, length), axis, 0, 0, tiled=True)
    return jnp.sum(blocks, axis=0)


def filled_with(value, identity):
    return jax.tree.map(
        lambda a, e: jnp.broadcast_to(jnp.asarray(e, a.dtype), a.shape), value, identity
    )


def gathered_once(value, axis):
    leaves = jax.tree.leaves(value)
    sequence = sorted(range(len(leaves)), key=lambda k: -leaves[k].size)
    width = (1, *leaves[sequence[0]].shape)[-1]
    lines = [
        jnp.pad(leaves[k].reshape(-1), (0, -leaves[k].size % width)).reshape(-1, width)
        for k in sequence
    ]
    both, at, found = (lax.all_gather(jnp.concatenate(lines), axis), 0, {})
    for k, line in zip(sequence, lines):
        section = both[:, at : at + len(line)].reshape(len(both), -1)
        found[k] = section[:, : leaves[k].size].reshape(-1, *leaves[k].shape)
        at += len(line)
    numbers = iter(range(len(leaves)))
    return jax.tree.map(lambda _: found[next(numbers)], value)


def carried_in(value, axes, combine, identity):
    before = start = filled_with(value, identity)
    running = value
    for axis in reversed(axes):
        length, index = (lax.axis_size(axis), lax.axis_index(axis))
        pieces = gathered_once(running, axis)
        inside, running = (start, start)
        for k in range(length):
            passed = k < index
            running = combine(running, jax.tree.map(lambda part: part[k], pieces))
            inside = jax.tree.map(lambda new, old: jnp.where(passed, new, old), running, inside)
        before = combine(inside, before)
    return before


def shifted(value, axis, by):
    length = lax.axis_size(axis)
    pairs = [(i, i + by) for i in range(length) if 0 <= i + by < length]
    return lax.ppermute(value, axis, pairs)


def sum_at_owner(value, axis, dim):
    length = lax.axis_size(axis)
    blocks = lax.all_to_all(split_up(value, dim, length), axis, 0, 0, tiled=True)
    return jnp.sum(blocks.astype(jnp.float32), axis=0)


def silu_slope(values):
    sigmoid = jax.nn.sigmoid(values)
    return sigmoid * (1.0 + values * (1.0 - sigmoid))


def project(left, weight):
    return jnp.dot(left, weight, preferred_element_type=jnp.float32).astype(jnp.bfloat16)


def normalize(retrieved, norm_gain):
    mean_square = jnp.mean(retrieved * retrieved, axis=-1, keepdims=True)
    return (retrieved * lax.rsqrt(mean_square + epsilon) * norm_gain).astype(jnp.bfloat16)


def lookup(table, chosen):
    matches = jnp.arange(table.shape[0], dtype=jnp.int32)[:, None] == chosen
    return jnp.sum(jnp.where(matches, table, 0.0), axis=0)


def as_columns(vector):
    return vector[..., None, :]


def as_rows(vector):
    return vector[..., :, None]


def compose(earlier, later):
    (
        prior_decay,
        prior_cross,
        prior_keep,
        prior_speed_in,
        prior_speed_out,
        prior_weight_in,
        prior_weight_out,
    ) = earlier
    (
        after_decay,
        after_cross,
        after_keep,
        after_speed_in,
        after_speed_out,
        after_weight_in,
        after_weight_out,
    ) = later
    decay = after_decay * prior_decay
    cross = after_cross * prior_decay + after_keep * prior_cross
    keep = after_keep * prior_keep
    speed_in = as_columns(after_decay) * prior_speed_in + after_speed_in
    speed_out = as_rows(after_decay) * prior_speed_out + after_speed_out
    weight_in = (
        as_columns(after_cross) * prior_speed_in
        + as_columns(after_keep) * prior_weight_in
        + after_weight_in
    )
    weight_out = (
        as_rows(after_cross) * prior_speed_out
        + as_rows(after_keep) * prior_weight_out
        + after_weight_out
    )
    return (decay, cross, keep, speed_in, speed_out, weight_in, weight_out)


def window_attend(query, keys, values, block_index):
    query_count = query.shape[0]
    key_count = keys.shape[0]
    span_rows = key_count - query_count
    distance = (
        span_rows
        + jnp.arange(query_count, dtype=jnp.int32)[:, None]
        - jnp.arange(key_count, dtype=jnp.int32)[None, :]
    )
    key_pos = (block_index * query_count - span_rows + jnp.arange(key_count, dtype=jnp.int32))[
        None, :
    ]
    allowed = (distance >= 0) & (distance < span_rows) & (key_pos >= 0)
    contexts = []
    for head_number in range(query.shape[1] // HEAD_DIM):
        low_col = head_number * HEAD_DIM
        scores = jnp.einsum(
            "qd,kd->qk",
            query[:, low_col : low_col + HEAD_DIM],
            keys[:, low_col : low_col + HEAD_DIM],
            preferred_element_type=jnp.float32,
        ) * HEAD_DIM ** (-0.5)
        scores = jnp.where(allowed, scores, -1e30)
        row_peak = jnp.max(scores, axis=-1, keepdims=True)
        weights = jnp.exp(scores - row_peak)
        probabilities = (weights / jnp.sum(weights, axis=-1, keepdims=True)).astype(jnp.bfloat16)
        contexts.append(
            jnp.dot(
                probabilities,
                values[:, low_col : low_col + HEAD_DIM],
                preferred_element_type=jnp.float32,
            ).astype(jnp.bfloat16)
        )
    return jnp.concatenate(contexts, axis=1)


def shards(
    tokens,
    mem_query_w,
    mem_key_w,
    mem_value_w,
    mem_in,
    mem_out,
    forget_levels,
    momentum_levels,
    step_levels,
    plan,
    norm_gain,
    attn_query_w,
    attn_key_w,
    attn_value_w,
    attn_out_w,
):
    tok_rows = tokens.shape[0]
    share_rows = tok_rows // lax.axis_size("head")
    my_start = lax.axis_index("head") * share_rows
    mem_query, mem_key, mem_value = (
        lax.all_gather(project(tokens, mem_query_w), "head", axis=1, tiled=True),
        lax.all_gather(project(tokens, mem_key_w), "head", axis=1, tiled=True),
        lax.all_gather(project(tokens, mem_value_w), "head", axis=1, tiled=True),
    )
    keys_wide = mem_key.astype(jnp.float32)
    pre_act = jnp.dot(keys_wide, mem_in)
    hidden = jax.nn.silu(pre_act)
    predicted = sent_and_summed(jnp.dot(hidden, mem_out), "head", 0)
    value_share = lax.dynamic_slice_in_dim(mem_value, my_start, share_rows, 0).astype(jnp.float32)
    residual_err = lax.all_gather(
        2.0 / tok_rows * (predicted - value_share), "head", axis=0, tiled=True
    )
    grad_out = jnp.dot(hidden.T, residual_err)
    slope_term = jnp.dot(residual_err, mem_out.T) * silu_slope(pre_act)
    grad_in = jnp.dot(keys_wide.T, slope_term)
    chosen = plan[0]
    forget = lookup(forget_levels, chosen)
    momentum = lookup(momentum_levels, chosen)
    step_rate = lookup(step_levels, chosen)
    change_in = -as_columns(step_rate) * grad_in
    change_out = -as_rows(step_rate) * grad_out
    element = (momentum, momentum, 1.0 - forget, change_in, change_out, change_in, change_out)
    identity = (
        jnp.ones_like(momentum),
        jnp.zeros_like(momentum),
        jnp.ones_like(momentum),
        jnp.zeros_like(grad_in),
        jnp.zeros_like(grad_out),
        jnp.zeros_like(grad_in),
        jnp.zeros_like(grad_out),
    )
    entering = carried_in(element, SEQ, compose, identity)
    weight_in = as_columns(entering[2]) * mem_in + entering[5]
    weight_out = as_rows(entering[2]) * mem_out + entering[6]
    query_hidden = jax.nn.silu(jnp.dot(mem_query.astype(jnp.float32), weight_in))
    retrieved = sent_and_summed(jnp.dot(query_hidden, weight_out), "head", 0)
    normed = lax.all_gather(normalize(retrieved, norm_gain), "head", axis=0, tiled=True)
    att_query = project(normed, attn_query_w)
    att_key = project(normed, attn_key_w)
    att_value = project(normed, attn_value_w)
    earlier = []
    for distance in range(SPAN, 0, -1):
        earlier.append(shifted((att_key, att_value), SEQ, distance))
    key_window = jnp.concatenate([received[0] for received in earlier] + [att_key], axis=0)
    value_window = jnp.concatenate([received[1] for received in earlier] + [att_value], axis=0)
    context = window_attend(att_query, key_window, value_window, lax.axis_index(SEQ))
    partial_out = jnp.dot(context, attn_out_w, preferred_element_type=jnp.float32)
    return sum_at_owner(partial_out.astype(jnp.bfloat16), "head", 1).astype(jnp.bfloat16)


def solution(mesh):
    split = Mesh(
        mesh.devices.reshape(4, 4, 2, mesh.shape["head"]), ("seq_0", "seq_1", "seq_2", "head")
    )
    in_specs = (
        P(SEQ, None),
        P(None, "head"),
        P(None, "head"),
        P(None, "head"),
        P(None, "head"),
        P("head", None),
        P(None, "head"),
        P(None, "head"),
        P(None, "head"),
        P(SEQ),
        P(),
        P(None, "head"),
        P(None, "head"),
        P(None, "head"),
        P("head", None),
    )
    out_specs = P(SEQ, "head")
    return jax.shard_map(
        shards, mesh=split, in_specs=in_specs, out_specs=out_specs, check_vma=False
    )
```

profile of v0, /device:TPU:33, one launch (start us, length us, event | category | flops | bytes accessed | tf_op | source)
XLA Modules:
  0.0 816.8 jit_solution(12139986413345933075)
XLA Ops:
  7.8 2.0 convolution_convert_fusion.5
  9.8 61.9 %all-gather.17.cloned.1.call-done = bf16[512,1024]{1,0:T(8,128)(2,1)} async-done(((bf16[512,128]{1,0:T(8,128)(2,1)}), bf16[512,1024]{1,0:T(8,128)(2,1)}) %all-gather.17.cloned.1.call-update) | async-done | bytes 1048592 | tf_op jit(solution)/shard_map/all_gather | solution.py:196
  71.7 1.8 fusion.357
  74.2 1.7 fusion.313
  76.0 3.7 all-to-all-start
  81.0 54.1 %all-to-all-done = f32[8,64,1024]{2,1,0:T(8,128)S(1)} async-done(((f32[8,64,1024]{2,1,0:T(8,128)}), f32[8,64,1024]{2,1,0:T(8,128)S(1)}, u32[]{:S(2)}, u32[]{:S(2)}) %all-to-all-start) | async-done | bytes 2097184 | tf_op jit(solution)/shard_map/all_to_all | solution.py:20
  135.3 23.0 %all-gather.19.cloned.1.call-done = bf16[512,1024]{1,0:T(8,128)(2,1)} async-done(((bf16[512,128]{1,0:T(8,128)(2,1)}), bf16[512,1024]{1,0:T(8,128)(2,1)}) %all-gather.19.cloned.1.call-update) | async-done | bytes 1048592 | tf_op jit(solution)/shard_map/all_gather | solution.py:197
  160.7 57.5 %all-gather.21.cloned.1.call-done = bf16[512,1024]{1,0:T(8,128)(2,1)} async-done(((bf16[64,1024]{1,0:T(8,128)(2,1)}), bf16[512,1024]{1,0:T(8,128)(2,1)}) %all-gather.21.cloned.1.call-update) | async-done | bytes 1048592 | tf_op jit(solution)/shard_map/all_gather | solution.py:204
  220.0 2.6 convolution_multiply_fusion
  222.7 4.1 concatenate.18
  226.8 17.6 %all-gather.25.cloned.1.call-done = f32[2,4099,128]{2,1,0:T(8,128)} async-done(((f32[1,4099,128]{2,1,0:T(8,128)}), f32[2,4099,128]{2,1,0:T(8,128)}) %all-gather.25.cloned.1.call-update) | async-done | bytes 4197392 | tf_op jit(solution)/shard_map/all_gather | solution.py:38
  249.3 2.1 bitcast_add_fusion.8
  251.5 4.1 concatenate.19
  255.6 154.2 %all-gather.27.cloned.1.call-done = f32[4,4099,128]{2,1,0:T(8,128)} async-done(((f32[1,4099,128]{2,1,0:T(8,128)}), f32[4,4099,128]{2,1,0:T(8,128)}) %all-gather.27.cloned.1.call-update) | async-done | bytes 8394768 | tf_op jit(solution)/shard_map/all_gather | solution.py:38
  413.4 2.3 fusion.37
  416.6 2.3 bitcast_add_fusion.4
  418.9 4.0 bitcast_add_fusion
  423.0 4.1 concatenate.20
  433.9 3.4 fusion.353
  437.3 1.9 squeeze.264
  439.2 2.0 squeeze.265
  446.6 65.9 %all-gather.29.cloned.1.call-done = f32[4,4099,128]{2,1,0:T(8,128)} async-done(((f32[1,4099,128]{2,1,0:T(8,128)}), f32[4,4099,128]{2,1,0:T(8,128)}) %all-gather.29.cloned.1.call-update) | async-done | bytes 8394768 | tf_op jit(solution)/shard_map/all_gather | solution.py:38
  512.5 3.4 fusion.352
  515.9 1.9 squeeze.256
  517.8 1.9 squeeze.257
  526.8 48.5 %all-gather.15.cloned.1.call-done = bf16[512,1024]{1,0:T(8,128)(2,1)} async-done(((bf16[512,128]{1,0:T(8,128)(2,1)}), bf16[512,1024]{1,0:T(8,128)(2,1)}) %all-gather.15.cloned.1.call-update) | async-done | bytes 1048592 | tf_op jit(solution)/shard_map/all_gather | solution.py:195
  575.3 11.3 %fusion.57 = f32[512,1024]{1,0:T(8,128)} fusion(f32[128,1024]{1,0:T(8,128)} %squeeze.275, f32[128,1024]{1,0:T(8,128)} %squeeze.274, f32[128,1024]{1,0:T(8,128)} %squeeze.273, f32[128,1024]{1,0:T(8,128)} %squeeze.272, f32[128,1024]{1,0:T(8,128)} %squeeze.271, f32[128,1024]{1,0:T(8,128)} %squeeze.270, f32[128,1024]{1,0:T(8,128)} %squeeze.269, ...), kind=kOutput, calls=%fused_computation.101 | convolution fusion | flops 287834112 | bytes 25205248 | tf_op jit(solution)/shard_map/dot_general | solution.py:230
  586.6 56.2 %all_to_all.15 = f32[8,64,1024]{2,1,0:T(8,128)S(1)} all-to-all(f32[8,64,1024]{2,1,0:T(8,128)} %bitcast.561), channel_id=1, replica_groups=mesh['seq_0'=4,'seq_1'=4,'seq_2'=2,'head'=8] {'head'}, dimensions={0} | all-to-all | bytes 4194304 | tf_op jit(solution)/shard_map/all_to_all | solution.py:20
  644.3 54.3 %all-gather.23.cloned.1.call-done = bf16[512,1024]{1,0:T(8,128)(2,1)} async-done(((bf16[64,1024]{1,0:T(8,128)(2,1)}), bf16[512,1024]{1,0:T(8,128)(2,1)}) %all-gather.23.cloned.1.call-update) | async-done | bytes 1048592 | tf_op jit(solution)/shard_map/all_gather | solution.py:231
  698.6 1.7 convolution_convert_fusion.2
  700.3 3.1 collective-permute-start
  703.5 5.4 collective-permute-start.1
  708.9 3.6 collective-permute-start.2
  713.8 4.1 collective-permute-start.4
  717.9 1.7 convolution_convert_fusion.3
  720.1 3.0 collective-permute-start.5
  723.1 2.3 collective-permute-start.6
  725.4 3.3 collective-permute-start.7
  731.5 8.3 %collective-permute-start.10 = (bf16[512,128]{1,0:T(8,128)(2,1)S(1)}, bf16[512,128]{1,0:T(8,128)(2,1)S(1)}, u32[]{:S(2)}, u32[]{:S(2)}) collective-permute-start(bf16[512,128]{1,0:T(8,128)(2,1)S(1)} %convolution_convert_fusion.1), channel_id=1, source_target_pairs={{0,48},{8,56},{16,64},{24,72},{32,80},{40,88},{48,96},{56,104},{64... | collective-permute-start | bytes 393224 | tf_op jit(solution)/shard_map/ppermute | solution.py:65
  739.8 2.8 collective-permute-start.11
  744.2 4.3 fusion.356
  748.5 4.2 fusion.355
  752.7 4.3 collective-permute-start.13
  757.1 2.0 collective-permute-start.14
  759.1 3.0 collective-permute-start.15
  766.8 1.9 fusion.16
  770.1 2.1 fusion.13
  773.0 36.1 %all_to_all.16 = bf16[8,512,128]{2,1,0:T(8,128)(2,1)S(1)} all-to-all(bf16[8,512,128]{2,1,0:T(8,128)(2,1)S(1)} %bitcast.560), channel_id=1, replica_groups=mesh['seq_0'=4,'seq_1'=4,'seq_2'=2,'head'=8] {'head'}, dimensions={0} | all-to-all | bytes 2097152 | tf_op jit(solution)/shard_map/all_to_all | solution.py:70
  (186 shorter events, 50.2 us)
Async XLA Ops:
  6.5 1.2 copy-start
  6.5 67.7 %copy-start.14 = (f32[128,1024]{1,0:T(8,128)S(1)}, f32[128,1024]{1,0:T(8,128)}, u32[]{:S(2)}) copy-start(f32[128,1024]{1,0:T(8,128)} %param.20) | copy-start | bytes 1572868
  6.5 65.2 %all-gather.17.cloned.1.call-start = ((), (), s32[]{:S(2)}) async-start(), calls=%async_computation.4 | async-start | bytes 1179648 | tf_op jit(solution)/shard_map/all_gather | solution.py:196
  76.0 3.8 copy-start.15
  76.0 59.1 %all-to-all-start = ((f32[8,64,1024]{2,1,0:T(8,128)}), f32[8,64,1024]{2,1,0:T(8,128)S(1)}, u32[]{:S(2)}, u32[]{:S(2)}) async-start(f32[8,64,1024]{2,1,0:T(8,128)} %bitcast.559), calls=%async_computation | async-start | bytes 4194304 | tf_op jit(solution)/shard_map/all_to_all | solution.py:20
  79.7 80.9 %copy-start.21 = (f32[16,128]{1,0:T(8,128)S(1)}, f32[16,128]{1,0:T(8,128)}, u32[]{:S(2)}) copy-start(f32[16,128]{1,0:T(8,128)} %param.21) | copy-start | bytes 24580
  79.7 80.9 %copy-start.22 = (f32[16,128]{1,0:T(8,128)S(1)}, f32[16,128]{1,0:T(8,128)}, u32[]{:S(2)}) copy-start(f32[16,128]{1,0:T(8,128)} %param.22) | copy-start | bytes 24580
  79.7 80.9 %copy-start.23 = (f32[16,128]{1,0:T(8,128)S(1)}, f32[16,128]{1,0:T(8,128)}, u32[]{:S(2)}) copy-start(f32[16,128]{1,0:T(8,128)} %param.23) | copy-start | bytes 24580
  79.8 78.5 %all-gather.19.cloned.1.call-start = ((), (), s32[]{:S(2)}) async-start(), calls=%async_computation.5 | async-start | bytes 1179648 | tf_op jit(solution)/shard_map/all_gather | solution.py:197
  80.9 137.3 %all-gather.21.cloned.1.call-start = ((), (), s32[]{:S(2)}) async-start(), calls=%async_computation.6 | async-start | bytes 1179648 | tf_op jit(solution)/shard_map/all_gather | solution.py:204
  135.2 84.8 %copy-start.11 = (bf16[512,1024]{1,0:T(8,128)(2,1)S(1)}, bf16[512,1024]{1,0:T(8,128)(2,1)}, u32[]{:S(2)}) copy-start(bf16[512,1024]{1,0:T(8,128)(2,1)} %all-gather.17.cloned.1.call-done) | copy-start | bytes 3145732
  159.8 60.2 %copy-start.13 = (f32[512,128]{1,0:T(8,128)S(1)}, f32[512,128]{1,0:T(8,128)}, u32[]{:S(2)}) copy-start(f32[512,128]{1,0:T(8,128)} %copy-done.12) | copy-start | bytes 786436
  159.8 84.5 %all-gather.25.cloned.1.call-start = ((), (), s32[]{:S(2)}) async-start(), calls=%async_computation.8 | async-start | bytes 6303744 | tf_op jit(solution)/shard_map/all_gather | solution.py:38
  226.8 183.1 %all-gather.27.cloned.1.call-start = ((), (), s32[]{:S(2)}) async-start(), calls=%async_computation.9 | async-start | bytes 10506240 | tf_op jit(solution)/shard_map/all_gather | solution.py:38
  248.5 7.0 copy-start.7
  248.5 7.0 copy-start.9
  255.6 256.9 %all-gather.29.cloned.1.call-start = ((), (), s32[]{:S(2)}) async-start(), calls=%async_computation.10 | async-start | bytes 10506240 | tf_op jit(solution)/shard_map/all_gather | solution.py:38
  415.7 3.2 copy-start.5
  415.7 7.2 copy-start.3
  418.9 8.2 %copy-start.10 = (f32[1024,128]{1,0:T(8,128)}, f32[1024,128]{1,0:T(8,128)S(1)}, u32[]{:S(2)}) copy-start(f32[1024,128]{1,0:T(8,128)S(1)} %get-tuple-element.46) | copy-start | bytes 1572868
  423.0 4.2 copy-start.16
  427.1 148.2 %all-gather.15.cloned.1.call-start = ((), (), s32[]{:S(2)}) async-start(), calls=%async_computation.3 | async-start | bytes 1179648 | tf_op jit(solution)/shard_map/all_gather | solution.py:195
  428.3 270.3 %all-gather.23.cloned.1.call-start = ((), (), s32[]{:S(2)}) async-start(), calls=%async_computation.7 | async-start | bytes 1179648 | tf_op jit(solution)/shard_map/all_gather | solution.py:231
  521.6 53.7 %copy-start.4 = (f32[1024,128]{1,0:T(8,128)S(1)}, f32[1024,128]{1,0:T(8,128)}, u32[]{:S(2)}) copy-start(f32[1024,128]{1,0:T(8,128)} %copy-done.3) | copy-start | bytes 1572868
  521.6 53.7 %copy-start.6 = (f32[1024,128]{1,0:T(8,128)S(1)}, f32[1024,128]{1,0:T(8,128)}, u32[]{:S(2)}) copy-start(f32[1024,128]{1,0:T(8,128)} %copy-done.5) | copy-start | bytes 1572868
  522.5 52.8 %copy-start.8 = (f32[1024,128]{1,0:T(8,128)S(1)}, f32[1024,128]{1,0:T(8,128)}, u32[]{:S(2)}) copy-start(f32[1024,128]{1,0:T(8,128)} %copy-done.7) | copy-start | bytes 1572868
  642.8 55.8 %copy-start.17 = (bf16[1024,128]{1,0:T(8,128)(2,1)S(1)}, bf16[1024,128]{1,0:T(8,128)(2,1)}, u32[]{:S(2)}) copy-start(bf16[1024,128]{1,0:T(8,128)(2,1)} %param.27) | copy-start | bytes 786436
  643.0 74.9 %copy-start.18 = (bf16[1024,128]{1,0:T(8,128)(2,1)S(1)}, bf16[1024,128]{1,0:T(8,128)(2,1)}, u32[]{:S(2)}) copy-start(bf16[1024,128]{1,0:T(8,128)(2,1)} %param.26) | copy-start | bytes 786436
  643.0 76.6 %copy-start.19 = (bf16[1024,128]{1,0:T(8,128)(2,1)S(1)}, bf16[1024,128]{1,0:T(8,128)(2,1)}, u32[]{:S(2)}) copy-start(bf16[1024,128]{1,0:T(8,128)(2,1)} %param.28) | copy-start | bytes 786436
  698.6 21.0 %copy-start.2 = (bf16[512,1024]{1,0:T(8,128)(2,1)S(1)}, bf16[512,1024]{1,0:T(8,128)(2,1)}, u32[]{:S(2)}) copy-start(bf16[512,1024]{1,0:T(8,128)(2,1)} %all-gather.23.cloned.1.call-done) | copy-start | bytes 3145732
  700.3 19.7 %collective-permute-start = (bf16[512,128]{1,0:T(8,128)(2,1)S(1)}, bf16[512,128]{1,0:T(8,128)(2,1)S(1)}, u32[]{:S(2)}, u32[]{:S(2)}) collective-permute-start(bf16[512,128]{1,0:T(8,128)(2,1)S(1)} %convolution_convert_fusion.2), channel_id=1, source_target_pairs={{0,64},{8,72},{16,80},{24,88},{32,96},{40,104},{48,112},{56,120},{... | collective-permute-start | bytes 393224 | tf_op jit(solution)/shard_map/ppermute | solution.py:65
  703.5 19.7 %collective-permute-start.1 = (bf16[512,128]{1,0:T(8,128)(2,1)S(1)}, bf16[512,128]{1,0:T(8,128)(2,1)S(1)}, u32[]{:S(2)}, u32[]{:S(2)}) collective-permute-start(bf16[512,128]{1,0:T(8,128)(2,1)S(1)} %convolution_convert_fusion.2), channel_id=1, source_target_pairs={{0,56},{8,64},{16,72},{24,80},{32,88},{40,96},{48,104},{56,112},{6... | collective-permute-start | bytes 393224 | tf_op jit(solution)/shard_map/ppermute | solution.py:65
  708.9 16.6 %collective-permute-start.2 = (bf16[512,128]{1,0:T(8,128)(2,1)S(1)}, bf16[512,128]{1,0:T(8,128)(2,1)S(1)}, u32[]{:S(2)}, u32[]{:S(2)}) collective-permute-start(bf16[512,128]{1,0:T(8,128)(2,1)S(1)} %convolution_convert_fusion.2), channel_id=1, source_target_pairs={{0,48},{8,56},{16,64},{24,72},{32,80},{40,88},{48,96},{56,104},{64... | collective-permute-start | bytes 393224 | tf_op jit(solution)/shard_map/ppermute | solution.py:65
  712.5 16.3 %collective-permute-start.3 = (bf16[512,128]{1,0:T(8,128)(2,1)S(1)}, bf16[512,128]{1,0:T(8,128)(2,1)S(1)}, u32[]{:S(2)}, u32[]{:S(2)}) collective-permute-start(bf16[512,128]{1,0:T(8,128)(2,1)S(1)} %convolution_convert_fusion.2), channel_id=1, source_target_pairs={{0,40},{8,48},{16,56},{24,64},{32,72},{40,80},{48,88},{56,96},{64,... | collective-permute-start | bytes 393224 | tf_op jit(solution)/shard_map/ppermute | solution.py:65
  713.8 16.3 %collective-permute-start.4 = (bf16[512,128]{1,0:T(8,128)(2,1)S(1)}, bf16[512,128]{1,0:T(8,128)(2,1)S(1)}, u32[]{:S(2)}, u32[]{:S(2)}) collective-permute-start(bf16[512,128]{1,0:T(8,128)(2,1)S(1)} %convolution_convert_fusion.2), channel_id=1, source_target_pairs={{0,32},{8,40},{16,48},{24,56},{32,64},{40,72},{48,80},{56,88},{64,... | collective-permute-start | bytes 393224 | tf_op jit(solution)/shard_map/ppermute | solution.py:65
  720.1 11.4 %collective-permute-start.5 = (bf16[512,128]{1,0:T(8,128)(2,1)S(1)}, bf16[512,128]{1,0:T(8,128)(2,1)S(1)}, u32[]{:S(2)}, u32[]{:S(2)}) collective-permute-start(bf16[512,128]{1,0:T(8,128)(2,1)S(1)} %convolution_convert_fusion.2), channel_id=1, source_target_pairs={{0,24},{8,32},{16,40},{24,48},{32,56},{40,64},{48,72},{56,80},{64,... | collective-permute-start | bytes 393224 | tf_op jit(solution)/shard_map/ppermute | solution.py:65
  723.1 16.6 %collective-permute-start.6 = (bf16[512,128]{1,0:T(8,128)(2,1)S(1)}, bf16[512,128]{1,0:T(8,128)(2,1)S(1)}, u32[]{:S(2)}, u32[]{:S(2)}) collective-permute-start(bf16[512,128]{1,0:T(8,128)(2,1)S(1)} %convolution_convert_fusion.2), channel_id=1, source_target_pairs={{0,16},{8,24},{16,32},{24,40},{32,48},{40,56},{48,64},{56,72},{64,... | collective-permute-start | bytes 393224 | tf_op jit(solution)/shard_map/ppermute | solution.py:65
  725.4 17.1 %collective-permute-start.7 = (bf16[512,128]{1,0:T(8,128)(2,1)S(1)}, bf16[512,128]{1,0:T(8,128)(2,1)S(1)}, u32[]{:S(2)}, u32[]{:S(2)}) collective-permute-start(bf16[512,128]{1,0:T(8,128)(2,1)S(1)} %convolution_convert_fusion.2), channel_id=1, source_target_pairs={{0,8},{8,16},{16,24},{24,32},{32,40},{40,48},{48,56},{56,64},{64,7... | collective-permute-start | bytes 393224 | tf_op jit(solution)/shard_map/ppermute | solution.py:65
  728.8 23.9 %collective-permute-start.8 = (bf16[512,128]{1,0:T(8,128)(2,1)S(1)}, bf16[512,128]{1,0:T(8,128)(2,1)S(1)}, u32[]{:S(2)}, u32[]{:S(2)}) collective-permute-start(bf16[512,128]{1,0:T(8,128)(2,1)S(1)} %convolution_convert_fusion.1), channel_id=1, source_target_pairs={{0,64},{8,72},{16,80},{24,88},{32,96},{40,104},{48,112},{56,120},{... | collective-permute-start | bytes 393224 | tf_op jit(solution)/shard_map/ppermute | solution.py:65
  730.1 26.9 %collective-permute-start.9 = (bf16[512,128]{1,0:T(8,128)(2,1)S(1)}, bf16[512,128]{1,0:T(8,128)(2,1)S(1)}, u32[]{:S(2)}, u32[]{:S(2)}) collective-permute-start(bf16[512,128]{1,0:T(8,128)(2,1)S(1)} %convolution_convert_fusion.1), channel_id=1, source_target_pairs={{0,56},{8,64},{16,72},{24,80},{32,88},{40,96},{48,104},{56,112},{6... | collective-permute-start | bytes 393224 | tf_op jit(solution)/shard_map/ppermute | solution.py:65
  731.5 27.6 %collective-permute-start.10 = (bf16[512,128]{1,0:T(8,128)(2,1)S(1)}, bf16[512,128]{1,0:T(8,128)(2,1)S(1)}, u32[]{:S(2)}, u32[]{:S(2)}) collective-permute-start(bf16[512,128]{1,0:T(8,128)(2,1)S(1)} %convolution_convert_fusion.1), channel_id=1, source_target_pairs={{0,48},{8,56},{16,64},{24,72},{32,80},{40,88},{48,96},{56,104},{64... | collective-permute-start | bytes 393224 | tf_op jit(solution)/shard_map/ppermute | solution.py:65
  739.8 22.3 %collective-permute-start.11 = (bf16[512,128]{1,0:T(8,128)(2,1)S(1)}, bf16[512,128]{1,0:T(8,128)(2,1)S(1)}, u32[]{:S(2)}, u32[]{:S(2)}) collective-permute-start(bf16[512,128]{1,0:T(8,128)(2,1)S(1)} %convolution_convert_fusion.1), channel_id=1, source_target_pairs={{0,40},{8,48},{16,56},{24,64},{32,72},{40,80},{48,88},{56,96},{64,... | collective-permute-start | bytes 393224 | tf_op jit(solution)/shard_map/ppermute | solution.py:65
  742.6 19.6 %collective-permute-start.12 = (bf16[512,128]{1,0:T(8,128)(2,1)S(1)}, bf16[512,128]{1,0:T(8,128)(2,1)S(1)}, u32[]{:S(2)}, u32[]{:S(2)}) collective-permute-start(bf16[512,128]{1,0:T(8,128)(2,1)S(1)} %convolution_convert_fusion.1), channel_id=1, source_target_pairs={{0,32},{8,40},{16,48},{24,56},{32,64},{40,72},{48,80},{56,88},{64,... | collective-permute-start | bytes 393224 | tf_op jit(solution)/shard_map/ppermute | solution.py:65
  752.7 9.5 %collective-permute-start.13 = (bf16[512,128]{1,0:T(8,128)(2,1)S(1)}, bf16[512,128]{1,0:T(8,128)(2,1)S(1)}, u32[]{:S(2)}, u32[]{:S(2)}) collective-permute-start(bf16[512,128]{1,0:T(8,128)(2,1)S(1)} %convolution_convert_fusion.1), channel_id=1, source_target_pairs={{0,24},{8,32},{16,40},{24,48},{32,56},{40,64},{48,72},{56,80},{64,... | collective-permute-start | bytes 393224 | tf_op jit(solution)/shard_map/ppermute | solution.py:65
  757.1 6.9 collective-permute-start.14
  759.1 6.2 collective-permute-start.15
  770.1 2.2 copy-start.20
  772.3 37.6 %copy-start.1 = (bf16[512,1024]{1,0:T(8,128)(2,1)S(1)}, bf16[512,1024]{1,0:T(8,128)(2,1)}, u32[]{:S(2)}) copy-start(bf16[512,1024]{1,0:T(8,128)(2,1)} %param.15) | copy-start | bytes 3145732
  (2 other events, 1.4 us)
Sparse Core Ops, SparseCore 0:
  9.9 61.7 all-gather.16
  83.1 75.1 all-gather.18
  160.9 57.3 all-gather.20
  226.9 17.4 all-gather.24
  255.7 154.1 all-gather.26
  427.3 85.1 all-gather.28
  515.0 60.2 all-gather.14
  644.4 54.1 all-gather.22
where the time goes:
time: 818 us; the launch traced here: 817 us
  waiting for transfers between devices  540 us (66%)
  blocking collectives  92.3 us (11%)
  starting transfers between devices  54.7 us (7%)
  local copies, waits for them, and re-layouts  47.1 us (6%)
  matrix products  40.3 us (5%)
  other arithmetic  27 us (3%)
  between operations  15.1 us (2%)
    all_gather x3, waiting for transfers between devices, gathered_once(): both, at, found = (lax.all_gather(jnp.concatenate(lines), axis), 0, {})  238 us
    all_gather x1, waiting for transfers between devices, shards(): lax.all_gather(project(tokens, mem_key_w), 'head', axis=1, tiled=True)  61.9 us
    all_gather x1, waiting for transfers between devices, shards(): lax.all_gather(2.0 / tok_rows * (predicted - value_share), 'head', axis=0...  57.5 us
    all_to_all x1, blocking collectives, sent_and_summed(): lax.all_to_all(split_up(value, dim, length), axis, 0, 0, tiled=True)  56.2 us
    all_gather x1, waiting for transfers between devices, shards(): lax.all_gather(normalize(retrieved, norm_gain), 'head', axis=0, tiled=True)  54.3 us
    all_to_all x1, waiting for transfers between devices, sent_and_summed(): lax.all_to_all(split_up(value, dim, length), axis, 0, 0, tiled=True)  54.1 us
    ppermute x16, starting transfers between devices, shifted(): return lax.ppermute(value, axis, pairs)  50.5 us
    all_gather x1, waiting for transfers between devices, shards(): lax.all_gather(project(tokens, mem_query_w), 'head', axis=1, tiled=True)  48.5 us
  transfers between devices with their start and end apart: 25, of which 11 were waited for; matrix products, arithmetic and copies ran while one was open for 6% of the time, Pallas kernels for 0%

commit v1 on v0

--- a/solution.py
+++ b/solution.py
@@ -192,7 +192,12 @@
     share_rows = tok_rows // lax.axis_size("head")
     my_start = lax.axis_index("head") * share_rows
     mem_query, mem_key, mem_value = (
-        lax.all_gather(project(tokens, mem_query_w), "head", axis=1, tiled=True),
+        jnp.concatenate(
+            lax.all_to_all(
+                jnp.stack([project(tokens, mem_query_w)] * lax.axis_size("head")), "head", 0, 0
+            ),
+            axis=1,
+        ),
         lax.all_gather(project(tokens, mem_key_w), "head", axis=1, tiled=True),
         lax.all_gather(project(tokens, mem_value_w), "head", axis=1, tiled=True),
     )

time: 818 us -> 776 us (0.949)
  waiting for transfers between devices: 540 us -> 484 us
    all_gather x1 -> x0, waiting for transfers between devices: 48.5 us -> none  [shards(): lax.all_gather(project(tokens, mem_query_w), 'head', axis=1, tiled=True)]
  transfers between devices with their start and end apart: 25 -> 25, of which waited for: 11 -> 10; matrix products, arithmetic and copies ran while one was open for 6% -> 6% of each run, Pallas kernels for 0% -> 0%
where the time goes in v1:
time: 776 us; the launch traced here: 774 us
  waiting for transfers between devices  484 us (62%)
  blocking collectives  98 us (13%)
  starting transfers between devices  61.2 us (8%)
  local copies, waits for them, and re-layouts  48.6 us (6%)
  matrix products  39.8 us (5%)
  other arithmetic  26.8 us (3%)
  between operations  15.1 us (2%)
    all_gather x3, waiting for transfers between devices, gathered_once(): both, at, found = (lax.all_gather(jnp.concatenate(lines), axis), 0, {})  230 us
    all_gather x1, waiting for transfers between devices, shards(): lax.all_gather(project(tokens, mem_key_w), 'head', axis=1, tiled=True)  61.9 us
    all_to_all x1, blocking collectives, sent_and_summed(): lax.all_to_all(split_up(value, dim, length), axis, 0, 0, tiled=True)  61.9 us
    all_gather x1, waiting for transfers between devices, shards(): lax.all_gather(2.0 / tok_rows * (predicted - value_share), 'head', axis=0...  57.5 us
    all_gather x1, waiting for transfers between devices, shards(): lax.all_gather(normalize(retrieved, norm_gain), 'head', axis=0, tiled=True)  54.4 us
    all_to_all x1, waiting for transfers between devices, sent_and_summed(): lax.all_to_all(split_up(value, dim, length), axis, 0, 0, tiled=True)  54.1 us
    ppermute x16, starting transfers between devices, shifted(): return lax.ppermute(value, axis, pairs)  50.5 us
    all_to_all x1, blocking collectives, sum_at_owner(): lax.all_to_all(split_up(value, dim, length), axis, 0, 0, tiled=True)  36.1 us
  transfers between devices with their start and end apart: 25, of which 10 were waited for; matrix products, arithmetic and copies ran while one was open for 6% of the time, Pallas kernels for 0%

profile of v1, /device:TPU:33, one launch (start us, length us, event | category | flops | bytes accessed | tf_op | source)
XLA Modules:
  0.0 774.1 jit_solution(9562553326930452772)
XLA Ops:
  7.8 2.0 convolution_convert_fusion.5
  9.8 61.9 %all-gather.14.cloned.1.call-done = bf16[512,1024]{1,0:T(8,128)(2,1)} async-done(((bf16[512,128]{1,0:T(8,128)(2,1)}), bf16[512,1024]{1,0:T(8,128)(2,1)}) %all-gather.14.cloned.1.call-update) | async-done | bytes 1048592 | tf_op jit(solution)/shard_map/all_gather | solution.py:201
  71.7 1.8 fusion.357
  74.2 1.8 fusion.313
  76.0 3.7 all-to-all-start.1
  81.0 54.1 %all-to-all-done.1 = f32[8,64,1024]{2,1,0:T(8,128)S(1)} async-done(((f32[8,64,1024]{2,1,0:T(8,128)}), f32[8,64,1024]{2,1,0:T(8,128)S(1)}, u32[]{:S(2)}, u32[]{:S(2)}) %all-to-all-start.1) | async-done | bytes 2097184 | tf_op jit(solution)/shard_map/all_to_all | solution.py:20
  135.3 23.0 %all-gather.16.cloned.1.call-done = bf16[512,1024]{1,0:T(8,128)(2,1)} async-done(((bf16[512,128]{1,0:T(8,128)(2,1)}), bf16[512,1024]{1,0:T(8,128)(2,1)}) %all-gather.16.cloned.1.call-update) | async-done | bytes 1048592 | tf_op jit(solution)/shard_map/all_gather | solution.py:202
  160.7 57.5 %all-gather.18.cloned.1.call-done = bf16[512,1024]{1,0:T(8,128)(2,1)} async-done(((bf16[64,1024]{1,0:T(8,128)(2,1)}), bf16[512,1024]{1,0:T(8,128)(2,1)}) %all-gather.18.cloned.1.call-update) | async-done | bytes 1048592 | tf_op jit(solution)/shard_map/all_gather | solution.py:209
  220.0 2.6 convolution_multiply_fusion
  222.7 4.1 concatenate.18
  226.8 17.6 %all-gather.22.cloned.1.call-done = f32[2,4099,128]{2,1,0:T(8,128)} async-done(((f32[1,4099,128]{2,1,0:T(8,128)}), f32[2,4099,128]{2,1,0:T(8,128)}) %all-gather.22.cloned.1.call-update) | async-done | bytes 4197392 | tf_op jit(solution)/shard_map/all_gather | solution.py:38
  249.4 2.1 bitcast_add_fusion.8
  251.5 4.1 concatenate.19
  255.6 154.2 %all-gather.24.cloned.1.call-done = f32[4,4099,128]{2,1,0:T(8,128)} async-done(((f32[1,4099,128]{2,1,0:T(8,128)}), f32[4,4099,128]{2,1,0:T(8,128)}) %all-gather.24.cloned.1.call-update) | async-done | bytes 8394768 | tf_op jit(solution)/shard_map/all_gather | solution.py:38
  413.4 2.3 fusion.37
  416.6 2.3 bitcast_add_fusion.4
  418.9 4.0 bitcast_add_fusion
  423.0 4.1 concatenate.20
  428.8 6.5 all-to-all-start
  440.8 3.9 fusion.353
  444.7 2.0 squeeze.264
  446.6 1.9 squeeze.265
  453.9 58.6 %all-gather.26.cloned.1.call-done = f32[4,4099,128]{2,1,0:T(8,128)} async-done(((f32[1,4099,128]{2,1,0:T(8,128)}), f32[4,4099,128]{2,1,0:T(8,128)}) %all-gather.26.cloned.1.call-update) | async-done | bytes 8394768 | tf_op jit(solution)/shard_map/all_gather | solution.py:38
  512.4 3.5 fusion.352
  515.9 1.9 squeeze.256
  517.8 1.9 squeeze.257
  526.7 11.5 %fusion.57 = f32[512,1024]{1,0:T(8,128)} fusion(f32[128,1024]{1,0:T(8,128)} %squeeze.275, f32[128,1024]{1,0:T(8,128)} %squeeze.274, f32[128,1024]{1,0:T(8,128)} %squeeze.273, f32[128,1024]{1,0:T(8,128)} %squeeze.272, f32[128,1024]{1,0:T(8,128)} %squeeze.271, f32[128,1024]{1,0:T(8,128)} %squeeze.270, f32[128,1024]{1,0:T(8,128)} %squeeze.269, ...), kind=kOutput, calls=%fused_computation.101 | convolution fusion | flops 287834112 | bytes 25205248 | tf_op jit(solution)/shard_map/dot_general | solution.py:235
  538.1 61.9 %all_to_all.20 = f32[8,64,1024]{2,1,0:T(8,128)S(1)} all-to-all(f32[8,64,1024]{2,1,0:T(8,128)} %bitcast.564), channel_id=1, replica_groups=mesh['seq_0'=4,'seq_1'=4,'seq_2'=2,'head'=8] {'head'}, dimensions={0} | all-to-all | bytes 4194304 | tf_op jit(solution)/shard_map/all_to_all | solution.py:20
  601.5 54.4 %all-gather.20.cloned.1.call-done = bf16[512,1024]{1,0:T(8,128)(2,1)} async-done(((bf16[64,1024]{1,0:T(8,128)(2,1)}), bf16[512,1024]{1,0:T(8,128)(2,1)}) %all-gather.20.cloned.1.call-update) | async-done | bytes 1048592 | tf_op jit(solution)/shard_map/all_gather | solution.py:236
  655.9 1.7 convolution_convert_fusion.2
  657.6 3.1 collective-permute-start
  660.8 5.4 collective-permute-start.1
  666.2 3.6 collective-permute-start.2
  671.1 4.1 collective-permute-start.4
  677.4 3.0 collective-permute-start.5
  680.4 2.3 collective-permute-start.6
  682.7 3.3 collective-permute-start.7
  688.8 8.3 %collective-permute-start.10 = (bf16[512,128]{1,0:T(8,128)(2,1)S(1)}, bf16[512,128]{1,0:T(8,128)(2,1)S(1)}, u32[]{:S(2)}, u32[]{:S(2)}) collective-permute-start(bf16[512,128]{1,0:T(8,128)(2,1)S(1)} %convolution_convert_fusion.1), channel_id=1, source_target_pairs={{0,48},{8,56},{16,64},{24,72},{32,80},{40,88},{48,96},{56,104},{64... | collective-permute-start | bytes 393224 | tf_op jit(solution)/shard_map/ppermute | solution.py:65
  697.1 2.8 collective-permute-start.11
  701.5 4.3 fusion.356
  705.8 4.2 fusion.355
  710.0 4.3 collective-permute-start.13
  714.4 2.0 collective-permute-start.14
  716.4 3.0 collective-permute-start.15
  719.5 1.7 collective-permute-done.14
  724.1 1.9 fusion.16
  727.5 2.1 fusion.13
  730.3 36.1 %all_to_all.21 = bf16[8,512,128]{2,1,0:T(8,128)(2,1)S(1)} all-to-all(bf16[8,512,128]{2,1,0:T(8,128)(2,1)S(1)} %bitcast.563), channel_id=1, replica_groups=mesh['seq_0'=4,'seq_1'=4,'seq_2'=2,'head'=8] {'head'}, dimensions={0} | all-to-all | bytes 2097152 | tf_op jit(solution)/shard_map/all_to_all | solution.py:70
  (187 shorter events, 50.6 us)
Async XLA Ops:
  6.5 1.2 copy-start
  6.5 67.7 %copy-start.14 = (f32[128,1024]{1,0:T(8,128)S(1)}, f32[128,1024]{1,0:T(8,128)}, u32[]{:S(2)}) copy-start(f32[128,1024]{1,0:T(8,128)} %param.20) | copy-start | bytes 1572868
  6.5 65.2 %all-gather.14.cloned.1.call-start = ((), (), s32[]{:S(2)}) async-start(), calls=%async_computation.4 | async-start | bytes 1179648 | tf_op jit(solution)/shard_map/all_gather | solution.py:201
  76.0 3.8 copy-start.15
  76.0 59.1 %all-to-all-start.1 = ((f32[8,64,1024]{2,1,0:T(8,128)}), f32[8,64,1024]{2,1,0:T(8,128)S(1)}, u32[]{:S(2)}, u32[]{:S(2)}) async-start(f32[8,64,1024]{2,1,0:T(8,128)} %bitcast.562), calls=%async_computation.1 | async-start | bytes 4194304 | tf_op jit(solution)/shard_map/all_to_all | solution.py:20
  79.7 80.9 %copy-start.21 = (f32[16,128]{1,0:T(8,128)S(1)}, f32[16,128]{1,0:T(8,128)}, u32[]{:S(2)}) copy-start(f32[16,128]{1,0:T(8,128)} %param.21) | copy-start | bytes 24580
  79.8 80.9 %copy-start.22 = (f32[16,128]{1,0:T(8,128)S(1)}, f32[16,128]{1,0:T(8,128)}, u32[]{:S(2)}) copy-start(f32[16,128]{1,0:T(8,128)} %param.22) | copy-start | bytes 24580
  79.8 80.9 %copy-start.23 = (f32[16,128]{1,0:T(8,128)S(1)}, f32[16,128]{1,0:T(8,128)}, u32[]{:S(2)}) copy-start(f32[16,128]{1,0:T(8,128)} %param.23) | copy-start | bytes 24580
  79.8 78.5 %all-gather.16.cloned.1.call-start = ((), (), s32[]{:S(2)}) async-start(), calls=%async_computation.5 | async-start | bytes 1179648 | tf_op jit(solution)/shard_map/all_gather | solution.py:202
  81.0 137.3 %all-gather.18.cloned.1.call-start = ((), (), s32[]{:S(2)}) async-start(), calls=%async_computation.6 | async-start | bytes 1179648 | tf_op jit(solution)/shard_map/all_gather | solution.py:209
  135.3 84.8 %copy-start.11 = (bf16[512,1024]{1,0:T(8,128)(2,1)S(1)}, bf16[512,1024]{1,0:T(8,128)(2,1)}, u32[]{:S(2)}) copy-start(bf16[512,1024]{1,0:T(8,128)(2,1)} %all-gather.14.cloned.1.call-done) | copy-start | bytes 3145732
  159.8 60.2 %copy-start.13 = (f32[512,128]{1,0:T(8,128)S(1)}, f32[512,128]{1,0:T(8,128)}, u32[]{:S(2)}) copy-start(f32[512,128]{1,0:T(8,128)} %copy-done.12) | copy-start | bytes 786436
  159.9 84.5 %all-gather.22.cloned.1.call-start = ((), (), s32[]{:S(2)}) async-start(), calls=%async_computation.8 | async-start | bytes 6303744 | tf_op jit(solution)/shard_map/all_gather | solution.py:38
  226.8 183.1 %all-gather.24.cloned.1.call-start = ((), (), s32[]{:S(2)}) async-start(), calls=%async_computation.9 | async-start | bytes 10506240 | tf_op jit(solution)/shard_map/all_gather | solution.py:38
  248.5 7.0 copy-start.7
  248.6 7.0 copy-start.9
  255.6 256.9 %all-gather.26.cloned.1.call-start = ((), (), s32[]{:S(2)}) async-start(), calls=%async_computation.10 | async-start | bytes 10506240 | tf_op jit(solution)/shard_map/all_gather | solution.py:38
  415.7 3.2 copy-start.5
  415.7 7.2 copy-start.3
  418.9 8.2 %copy-start.10 = (f32[1024,128]{1,0:T(8,128)}, f32[1024,128]{1,0:T(8,128)S(1)}, u32[]{:S(2)}) copy-start(f32[1024,128]{1,0:T(8,128)S(1)} %get-tuple-element.46) | copy-start | bytes 1572868
  423.0 4.1 copy-start.16
  428.8 97.9 %all-to-all-start = ((bf16[8,512,128]{1,2,0:T(8,128)(2,1)}), bf16[8,512,128]{1,2,0:T(8,128)(2,1)}, u32[]{:S(2)}, u32[]{:S(2)}) async-start(bf16[8,512,128]{1,2,0:T(8,128)(2,1)} %stack.2), calls=%async_computation | async-start | bytes 2097152 | tf_op jit(solution)/shard_map/all_to_all | solution.py:196
  435.2 220.6 %all-gather.20.cloned.1.call-start = ((), (), s32[]{:S(2)}) async-start(), calls=%async_computation.7 | async-start | bytes 1179648 | tf_op jit(solution)/shard_map/all_gather | solution.py:236
  521.5 5.1 copy-start.4
  521.5 5.1 copy-start.6
  522.4 4.2 copy-start.8
  600.0 55.9 %copy-start.17 = (bf16[1024,128]{1,0:T(8,128)(2,1)S(1)}, bf16[1024,128]{1,0:T(8,128)(2,1)}, u32[]{:S(2)}) copy-start(bf16[1024,128]{1,0:T(8,128)(2,1)} %param.27) | copy-start | bytes 786436
  600.2 75.0 %copy-start.18 = (bf16[1024,128]{1,0:T(8,128)(2,1)S(1)}, bf16[1024,128]{1,0:T(8,128)(2,1)}, u32[]{:S(2)}) copy-start(bf16[1024,128]{1,0:T(8,128)(2,1)} %param.26) | copy-start | bytes 786436
  600.2 76.7 %copy-start.19 = (bf16[1024,128]{1,0:T(8,128)(2,1)S(1)}, bf16[1024,128]{1,0:T(8,128)(2,1)}, u32[]{:S(2)}) copy-start(bf16[1024,128]{1,0:T(8,128)(2,1)} %param.28) | copy-start | bytes 786436
  655.9 21.0 %copy-start.2 = (bf16[512,1024]{1,0:T(8,128)(2,1)S(1)}, bf16[512,1024]{1,0:T(8,128)(2,1)}, u32[]{:S(2)}) copy-start(bf16[512,1024]{1,0:T(8,128)(2,1)} %all-gather.20.cloned.1.call-done) | copy-start | bytes 3145732
  657.6 19.7 %collective-permute-start = (bf16[512,128]{1,0:T(8,128)(2,1)S(1)}, bf16[512,128]{1,0:T(8,128)(2,1)S(1)}, u32[]{:S(2)}, u32[]{:S(2)}) collective-permute-start(bf16[512,128]{1,0:T(8,128)(2,1)S(1)} %convolution_convert_fusion.2), channel_id=1, source_target_pairs={{0,64},{8,72},{16,80},{24,88},{32,96},{40,104},{48,112},{56,120},{... | collective-permute-start | bytes 393224 | tf_op jit(solution)/shard_map/ppermute | solution.py:65
  660.8 19.7 %collective-permute-start.1 = (bf16[512,128]{1,0:T(8,128)(2,1)S(1)}, bf16[512,128]{1,0:T(8,128)(2,1)S(1)}, u32[]{:S(2)}, u32[]{:S(2)}) collective-permute-start(bf16[512,128]{1,0:T(8,128)(2,1)S(1)} %convolution_convert_fusion.2), channel_id=1, source_target_pairs={{0,56},{8,64},{16,72},{24,80},{32,88},{40,96},{48,104},{56,112},{6... | collective-permute-start | bytes 393224 | tf_op jit(solution)/shard_map/ppermute | solution.py:65
  666.2 16.6 %collective-permute-start.2 = (bf16[512,128]{1,0:T(8,128)(2,1)S(1)}, bf16[512,128]{1,0:T(8,128)(2,1)S(1)}, u32[]{:S(2)}, u32[]{:S(2)}) collective-permute-start(bf16[512,128]{1,0:T(8,128)(2,1)S(1)} %convolution_convert_fusion.2), channel_id=1, source_target_pairs={{0,48},{8,56},{16,64},{24,72},{32,80},{40,88},{48,96},{56,104},{64... | collective-permute-start | bytes 393224 | tf_op jit(solution)/shard_map/ppermute | solution.py:65
  669.8 16.3 %collective-permute-start.3 = (bf16[512,128]{1,0:T(8,128)(2,1)S(1)}, bf16[512,128]{1,0:T(8,128)(2,1)S(1)}, u32[]{:S(2)}, u32[]{:S(2)}) collective-permute-start(bf16[512,128]{1,0:T(8,128)(2,1)S(1)} %convolution_convert_fusion.2), channel_id=1, source_target_pairs={{0,40},{8,48},{16,56},{24,64},{32,72},{40,80},{48,88},{56,96},{64,... | collective-permute-start | bytes 393224 | tf_op jit(solution)/shard_map/ppermute | solution.py:65
  671.1 16.3 %collective-permute-start.4 = (bf16[512,128]{1,0:T(8,128)(2,1)S(1)}, bf16[512,128]{1,0:T(8,128)(2,1)S(1)}, u32[]{:S(2)}, u32[]{:S(2)}) collective-permute-start(bf16[512,128]{1,0:T(8,128)(2,1)S(1)} %convolution_convert_fusion.2), channel_id=1, source_target_pairs={{0,32},{8,40},{16,48},{24,56},{32,64},{40,72},{48,80},{56,88},{64,... | collective-permute-start | bytes 393224 | tf_op jit(solution)/shard_map/ppermute | solution.py:65
  677.4 11.4 %collective-permute-start.5 = (bf16[512,128]{1,0:T(8,128)(2,1)S(1)}, bf16[512,128]{1,0:T(8,128)(2,1)S(1)}, u32[]{:S(2)}, u32[]{:S(2)}) collective-permute-start(bf16[512,128]{1,0:T(8,128)(2,1)S(1)} %convolution_convert_fusion.2), channel_id=1, source_target_pairs={{0,24},{8,32},{16,40},{24,48},{32,56},{40,64},{48,72},{56,80},{64,... | collective-permute-start | bytes 393224 | tf_op jit(solution)/shard_map/ppermute | solution.py:65
  680.4 16.6 %collective-permute-start.6 = (bf16[512,128]{1,0:T(8,128)(2,1)S(1)}, bf16[512,128]{1,0:T(8,128)(2,1)S(1)}, u32[]{:S(2)}, u32[]{:S(2)}) collective-permute-start(bf16[512,128]{1,0:T(8,128)(2,1)S(1)} %convolution_convert_fusion.2), channel_id=1, source_target_pairs={{0,16},{8,24},{16,32},{24,40},{32,48},{40,56},{48,64},{56,72},{64,... | collective-permute-start | bytes 393224 | tf_op jit(solution)/shard_map/ppermute | solution.py:65
  682.7 17.2 %collective-permute-start.7 = (bf16[512,128]{1,0:T(8,128)(2,1)S(1)}, bf16[512,128]{1,0:T(8,128)(2,1)S(1)}, u32[]{:S(2)}, u32[]{:S(2)}) collective-permute-start(bf16[512,128]{1,0:T(8,128)(2,1)S(1)} %convolution_convert_fusion.2), channel_id=1, source_target_pairs={{0,8},{8,16},{16,24},{24,32},{32,40},{40,48},{48,56},{56,64},{64,7... | collective-permute-start | bytes 393224 | tf_op jit(solution)/shard_map/ppermute | solution.py:65
  686.1 23.9 %collective-permute-start.8 = (bf16[512,128]{1,0:T(8,128)(2,1)S(1)}, bf16[512,128]{1,0:T(8,128)(2,1)S(1)}, u32[]{:S(2)}, u32[]{:S(2)}) collective-permute-start(bf16[512,128]{1,0:T(8,128)(2,1)S(1)} %convolution_convert_fusion.1), channel_id=1, source_target_pairs={{0,64},{8,72},{16,80},{24,88},{32,96},{40,104},{48,112},{56,120},{... | collective-permute-start | bytes 393224 | tf_op jit(solution)/shard_map/ppermute | solution.py:65
  687.4 26.9 %collective-permute-start.9 = (bf16[512,128]{1,0:T(8,128)(2,1)S(1)}, bf16[512,128]{1,0:T(8,128)(2,1)S(1)}, u32[]{:S(2)}, u32[]{:S(2)}) collective-permute-start(bf16[512,128]{1,0:T(8,128)(2,1)S(1)} %convolution_convert_fusion.1), channel_id=1, source_target_pairs={{0,56},{8,64},{16,72},{24,80},{32,88},{40,96},{48,104},{56,112},{6... | collective-permute-start | bytes 393224 | tf_op jit(solution)/shard_map/ppermute | solution.py:65
  688.8 27.6 %collective-permute-start.10 = (bf16[512,128]{1,0:T(8,128)(2,1)S(1)}, bf16[512,128]{1,0:T(8,128)(2,1)S(1)}, u32[]{:S(2)}, u32[]{:S(2)}) collective-permute-start(bf16[512,128]{1,0:T(8,128)(2,1)S(1)} %convolution_convert_fusion.1), channel_id=1, source_target_pairs={{0,48},{8,56},{16,64},{24,72},{32,80},{40,88},{48,96},{56,104},{64... | collective-permute-start | bytes 393224 | tf_op jit(solution)/shard_map/ppermute | solution.py:65
  697.1 22.3 %collective-permute-start.11 = (bf16[512,128]{1,0:T(8,128)(2,1)S(1)}, bf16[512,128]{1,0:T(8,128)(2,1)S(1)}, u32[]{:S(2)}, u32[]{:S(2)}) collective-permute-start(bf16[512,128]{1,0:T(8,128)(2,1)S(1)} %convolution_convert_fusion.1), channel_id=1, source_target_pairs={{0,40},{8,48},{16,56},{24,64},{32,72},{40,80},{48,88},{56,96},{64,... | collective-permute-start | bytes 393224 | tf_op jit(solution)/shard_map/ppermute | solution.py:65
  699.9 19.6 %collective-permute-start.12 = (bf16[512,128]{1,0:T(8,128)(2,1)S(1)}, bf16[512,128]{1,0:T(8,128)(2,1)S(1)}, u32[]{:S(2)}, u32[]{:S(2)}) collective-permute-start(bf16[512,128]{1,0:T(8,128)(2,1)S(1)} %convolution_convert_fusion.1), channel_id=1, source_target_pairs={{0,32},{8,40},{16,48},{24,56},{32,64},{40,72},{48,80},{56,88},{64,... | collective-permute-start | bytes 393224 | tf_op jit(solution)/shard_map/ppermute | solution.py:65
  710.0 9.5 %collective-permute-start.13 = (bf16[512,128]{1,0:T(8,128)(2,1)S(1)}, bf16[512,128]{1,0:T(8,128)(2,1)S(1)}, u32[]{:S(2)}, u32[]{:S(2)}) collective-permute-start(bf16[512,128]{1,0:T(8,128)(2,1)S(1)} %convolution_convert_fusion.1), channel_id=1, source_target_pairs={{0,24},{8,32},{16,40},{24,48},{32,56},{40,64},{48,72},{56,80},{64,... | collective-permute-start | bytes 393224 | tf_op jit(solution)/shard_map/ppermute | solution.py:65
  714.4 6.9 collective-permute-start.14
  716.4 6.2 collective-permute-start.15
  727.4 2.2 copy-start.20
  729.6 37.6 %copy-start.1 = (bf16[512,1024]{1,0:T(8,128)(2,1)S(1)}, bf16[512,1024]{1,0:T(8,128)(2,1)}, u32[]{:S(2)}) copy-start(bf16[512,1024]{1,0:T(8,128)(2,1)} %param.15) | copy-start | bytes 3145732
  (2 other events, 1.4 us)
Sparse Core Ops, SparseCore 0:
  9.9 61.7 all-gather.13
  83.1 75.1 all-gather.15
  160.9 57.3 all-gather.17
  226.9 17.4 all-gather.21
  255.7 154.1 all-gather.23
  427.2 85.1 all-gather.25
  601.6 54.2 all-gather.19
